TPU v7x, 32 devices: a whole 2x2x4 slice. The times are simulated.
32 devices in a mesh: mem: 4 (over x, core), lat: 8 (over z, y).
Axes of the slice: x: 2, y: 2, z: 4, core: 2. Of those that a mesh axis runs over, the one named last changes fastest.
Arguments:
- control: bfloat16 [8, 10, 704, 1440], P('mem', None, 'lat'), may hold values from -6 to 6
- perturb: bfloat16 [8, 10, 704, 1440], P('mem', None, None, 'lat'), may hold values from -6 to 6
- lon_loc: bfloat16 [1440, 1440], P(None, 'mem'), may hold values from 0 to 1, as said below
- lat_loc: bfloat16 [704, 704], P('mem'), may hold values from 0 to 1, as said below
- static_scale: float32 [10, 704, 1440], P(None, 'mem', 'lat'), may hold values from 0.3 to 1
- static_field: float32 [10, 704, 1440], P(None, 'mem', 'lat'), may hold values from -6 to 6
- courant: float32 [2, 704, 1440], P(None, 'mem', 'lat'), may hold values from -0.48 to 0.48
Outputs:
- increment: float32 [10, 704, 1440], P(None, 'mem', 'lat')
- evolved: float32 [10, 704, 1440], P(None, 'mem', 'lat')
Inputs may be any that keep to these rules, and one draw needn't show every extreme that they name: `lon_loc`: Symmetric, with positive entries. `lat_loc`: Symmetric, with positive entries.
All inputs are finite; a program needn't handle non-finite values.
Results may differ from a plain program's by a relative error of at most 0.0027.
Values may be sent and summed in bfloat16 or wider, within the bound.
No kernel may reach another device: no remote copies, remote signals or barrier semaphores. Data moves between devices by JAX's collectives and lax.ppermute only.
A program may use at most 128 MiB of HBM per device.

v0:
```python
import math
import jax
import jax.numpy as jnp
from jax import lax
from jax.sharding import PartitionSpec as P

NLAT = 704
STEPS = 4


def padded_2(shard, sides, width, wrap):
    for axis, dim in sides:
        size, length = (lax.axis_size(axis), shard.shape[dim])
        up = [(i, (i + 1) % size) for i in range(size if wrap else size - 1)]
        down = [(j, i) for i, j in up]
        last = lax.slice_in_dim(shard, length - width, length, axis=dim)
        leading = lax.slice_in_dim(shard, 0, width, axis=dim)
        before = lax.ppermute(last, axis, up)
        after = lax.ppermute(leading, axis, down)
        shard = jnp.concatenate([before, shard, after], axis=dim)
    return shard


def upwind(padded, east_west, north_south):
    center = padded[:, 1:-1, 1:-1]
    western = padded[:, 1:-1, :-2]
    eastern = padded[:, 1:-1, 2:]
    southern = padded[:, :-2, 1:-1]
    northern = padded[:, 2:, 1:-1]
    zonal = jnp.maximum(east_west, 0.0) * (center - western) + jnp.minimum(east_west, 0.0) * (
        eastern - center
    )
    meridional = jnp.maximum(north_south, 0.0) * (center - southern) + jnp.minimum(
        north_south, 0.0
    ) * (northern - center)
    return center - zonal - meridional


def lon_rim(values, width):
    return padded_2(values, (("lat", 2),), width, True)


def lat_rim(values, width):
    return padded_2(values, (("mem", 1),), width, False)


def evolve(current, courant):
    fields = current.shape[0]
    stacked = jnp.concatenate([current, courant], axis=0)
    extended = lat_rim(lon_rim(stacked, STEPS), STEPS)
    result = extended[:fields]
    wind_ext = extended[fields:]
    for step_index in range(STEPS):
        margin = step_index + 1
        inner_wind = wind_ext[
            :, margin : wind_ext.shape[1] - margin, margin : wind_ext.shape[2] - margin
        ]
        result = upwind(result, inner_wind[0], inner_wind[1])
    return result


def per_device(control, perturb, lon_loc, lat_loc, static_scale, static_field, courant):
    along_lon = jnp.einsum(
        "mfal,lc->amfc",
        control,
        lax.all_gather(lon_loc, "mem", axis=1, tiled=True),
        preferred_element_type=jnp.float32,
    ).astype(jnp.bfloat16)
    banded = lax.all_to_all(along_lon, "lat", split_axis=3, concat_axis=0, tiled=True)
    mem_here = banded.shape[1]
    fields = banded.shape[2]
    lon_width = banded.shape[3]
    flat_band = banded.reshape(banded.shape[0], mem_here * fields * lon_width)
    pert_rows = jnp.transpose(perturb, (2, 0, 1, 3))
    lat_weights_all = lax.all_gather(lat_loc, "mem", axis=0, tiled=True)
    members = mem_here * lax.axis_size("mem")
    ens_scale = 1.0 / math.sqrt(members - 1)
    rows_own = NLAT // lax.axis_size("mem")
    localized = jnp.dot(lat_weights_all, flat_band, preferred_element_type=jnp.float32)
    localized = localized.reshape(NLAT, mem_here, fields, lon_width)
    ensemble_all = jnp.transpose(
        lax.psum(jnp.sum(localized * pert_rows.astype(jnp.float32), axis=1) * ens_scale, "mem"),
        (1, 0, 2),
    )
    offset = lax.axis_index("mem") * rows_own
    ensemble = lax.dynamic_slice_in_dim(ensemble_all, offset, rows_own, 1)
    increment = ensemble + static_scale * static_field
    evolved = evolve(increment, courant)
    return (increment, evolved)


def solution(mesh):
    placed = (
        P("mem", None, "lat", None),
        P("mem", None, None, "lat"),
        P(None, "mem"),
        P("mem", None),
        P(None, "mem", "lat"),
        P(None, "mem", "lat"),
        P(None, "mem", "lat"),
    )
    return jax.shard_map(
        per_device,
        mesh=mesh,
        in_specs=placed,
        out_specs=(P(None, "mem", "lat"), P(None, "mem", "lat")),
        check_vma=False,
    )
```

profile of v0, /device:TPU:1, one launch (start us, length us, event | category | flops | bytes accessed | tf_op | source)
XLA Modules:
  0.0 472.6 jit_solution(8537434043374464706)
XLA Ops:
  7.2 2.4 copy.32
  9.6 38.8 %all-gather.2.cloned.1.call-done = bf16[1440,1440]{0,1:T(8,128)(2,1)} async-done(((bf16[1440,360]{0,1:T(8,128)(2,1)}), bf16[1440,1440]{0,1:T(8,128)(2,1)}) %all-gather.2.cloned.1.call-update) | async-done | bytes 4147216 | tf_op jit(solution)/shard_map/all_gather | solution.py:66
  48.4 13.5 %convert_bitcast_fusion = bf16[88,2,10,1440]{3,0,2,1:T(8,128)(2,1)} fusion(bf16[2,10,88,1440]{3,2,1,0:T(8,128)(2,1)} %param.7, bf16[1440,1440]{0,1:T(8,128)(2,1)} %all-gather.2.cloned.1.call-done), kind=kOutput, calls=%fused_computation.4 | convolution fusion | flops 7301606400 | bytes 14284800 | tf_op jit(solution)/shard_map/mfal,lc->amfc/dot_general | solution.py:63
  61.8 16.8 %copy.34 = bf16[88,2,10,1440]{0,1,2,3:T(2,128)(2,1)} copy(bf16[88,2,10,1440]{3,0,2,1:T(8,128)(2,1)} %convert_bitcast_fusion) | data formatting | bytes 10137600 | tf_op jit(solution)/shard_map/convert_element_type | solution.py:68
  78.6 5.4 %all-to-all-start = ((bf16[88,2,10,1440]{0,1,2,3:T(2,128)(2,1)}), bf16[88,2,10,1440]{0,1,2,3:T(2,128)(2,1)}, u32[]{:S(2)}, u32[]{:S(2)}) async-start(bf16[88,2,10,1440]{0,1,2,3:T(2,128)(2,1)} %copy.34), calls=%async_computation | async-start | bytes 14745600 | tf_op jit(solution)/shard_map/all_to_all | solution.py:69
  84.0 10.5 %all_gather.7 = bf16[704,704]{1,0:T(8,128)(2,1)S(1)} all-gather(bf16[176,704]{1,0:T(8,128)(2,1)S(1)} %copy-done.7), channel_id=1, replica_groups=mesh['mem'=4,'lat'=8] {'mem'}, dimensions={0}, use_global_device_ids=true | all-gather | bytes 1239040 | tf_op jit(solution)/shard_map/all_gather | solution.py:75
  94.5 150.4 %all-to-all-done = bf16[88,2,10,1440]{0,1,2,3:T(2,128)(2,1)} async-done(((bf16[88,2,10,1440]{0,1,2,3:T(2,128)(2,1)}), bf16[88,2,10,1440]{0,1,2,3:T(2,128)(2,1)}, u32[]{:S(2)}, u32[]{:S(2)}) %all-to-all-start) | async-done | bytes 5068832 | tf_op jit(solution)/shard_map/all_to_all | solution.py:69
  245.0 8.0 %copy.59 = bf16[88,2,10,8,180]{0,3,4,2,1:T(8,128)(2,1)} copy(bf16[88,2,10,8,180]{0,1,2,4,3:T(2,128)(2,1)} %bitcast.2) | data formatting | bytes 10137600 | tf_op jit(solution)/shard_map/all_to_all | solution.py:69
  253.0 12.2 %reshape.11 = bf16[704,3600]{0,1:T(8,128)(2,1)} reshape(bf16[8,88,2,10,180]{1,0,4,3,2:T(8,128)(2,1)} %bitcast.58) | data formatting | bytes 10137600 | tf_op jit(solution)/shard_map/reshape | solution.py:73
  265.2 9.6 %convolution_bitcast_fusion = f32[704,3600]{1,0:T(8,128)} fusion(bf16[704,3600]{0,1:T(8,128)(2,1)} %reshape.11, bf16[704,704]{1,0:T(8,128)(2,1)S(1)} %all_gather.7), kind=kOutput, calls=%fused_computation.3 | convolution fusion | flops 3568435200 | bytes 16197632 | tf_op jit(solution)/shard_map/dot_general | solution.py:79
  274.7 11.8 %copy.36 = f32[704,3600]{0,1:T(8,128)} copy(f32[704,3600]{1,0:T(8,128)} %convolution_bitcast_fusion) | data formatting | bytes 20275200 | tf_op jit(solution)/shard_map/dot_general | solution.py:79
  286.6 11.6 %reshape.12 = f32[704,2,10,180]{0,3,2,1:T(8,128)} reshape(f32[704,3600]{0,1:T(8,128)} %copy.36) | data formatting | bytes 20275200 | tf_op jit(solution)/shard_map/reshape | solution.py:80
  298.1 10.3 %fusion = f32[704,10,180]{0,2,1:T(8,128)} fusion(f32[704,2,10,180]{0,3,2,1:T(8,128)} %reshape.12, bf16[2,10,704,180]{2,0,3,1:T(2,128)(2,1)} %param.8), kind=kLoop, calls=%fused_computation.1 | loop fusion | flops 6336000 | bytes 20275200 | tf_op jit(solution)/shard_map/reduce_sum | solution.py:82
  308.4 5.5 %broadcast_multiply_fusion = f32[704,10,180]{0,2,1:T(8,128)} fusion(f32[704,10,180]{0,2,1:T(8,128)} %fusion), kind=kLoop, calls=%fused_computation.6 | loop fusion | flops 1267200 | bytes 10137600 | tf_op jit(solution)/shard_map/mul | solution.py:82
  314.0 1.5 copy-done.1
  315.4 1.8 copy.38
  317.3 3.0 copy.39
  320.5 101.5 %all-reduce.2.cloned.1.call-done = f32[704,10,180]{0,2,1:T(8,128)} async-done(((f32[704,10,180]{0,2,1:T(8,128)}), f32[704,10,180]{0,2,1:T(8,128)}) %all-reduce.2.cloned.1.call-update) | async-done | bytes 5068816 | tf_op jit(solution)/shard_map/psum | solution.py:82
  422.0 3.5 bitcast_add_fusion
  426.8 3.0 collective-permute-start.1
  429.8 1.6 collective-permute-done
  431.8 1.4 fusion.34
  433.2 2.4 copy.45
  435.6 4.1 collective-permute-start.2
  440.8 2.1 collective-permute-start.3
  447.2 1.8 copy.53
  450.3 2.2 copy.48
  455.6 2.1 fusion.4
  457.7 2.0 fusion.28
  459.8 2.0 fusion.20
  461.8 2.1 fusion.12
  463.9 1.8 copy.54
  (44 shorter events, 11.5 us)
Async XLA Ops:
  7.2 41.2 %all-gather.2.cloned.1.call-start = ((), (), s32[]{:S(2)}) async-start(), calls=%async_computation.1 | async-start | bytes 5529600 | tf_op jit(solution)/shard_map/all_gather | solution.py:66
  78.6 5.4 %copy-start.7 = (bf16[176,704]{1,0:T(8,128)(2,1)S(1)}, bf16[176,704]{1,0:T(8,128)(2,1)}, u32[]{:S(2)}) copy-start(bf16[176,704]{1,0:T(8,128)(2,1)} %param.10) | copy-start | bytes 743428
  78.6 166.4 %all-to-all-start = ((bf16[88,2,10,1440]{0,1,2,3:T(2,128)(2,1)}), bf16[88,2,10,1440]{0,1,2,3:T(2,128)(2,1)}, u32[]{:S(2)}, u32[]{:S(2)}) async-start(bf16[88,2,10,1440]{0,1,2,3:T(2,128)(2,1)} %copy.34), calls=%async_computation | async-start | bytes 14745600 | tf_op jit(solution)/shard_map/all_to_all | solution.py:69
  84.0 338.0 %all-reduce.2.cloned.1.call-start = ((), (), s32[]{:S(2)}) async-start(), calls=%async_computation.2 | async-start | bytes 11304960 | tf_op jit(solution)/shard_map/psum | solution.py:82
  313.9 1.5 copy-start.1
  317.3 3.0 copy-start.2
  425.6 5.9 %collective-permute-start = (f32[12,176,4]{1,0,2:T(8,128)S(1)}, f32[12,176,4]{1,0,2:T(8,128)S(1)}, u32[]{:S(2)}, u32[]{:S(2)}) collective-permute-start(f32[12,176,4]{1,0,2:T(8,128)S(1)} %copy.41), channel_id=1, source_target_pairs={{0,1},{1,2},{2,3},{3,4},{4,5},{5,6},{6,7},{7,0},{8,9},{9,10},{10,1... | collective-permute-start | bytes 101384 | tf_op jit(solution)/shard_map/ppermute | solution.py:18
  426.8 4.7 collective-permute-start.1
  435.6 13.4 %collective-permute-start.2 = (f32[12,4,188]{2,1,0:T(4,128)}, f32[12,4,188]{2,1,0:T(4,128)}, u32[]{:S(2)}, u32[]{:S(2)}) collective-permute-start(f32[12,4,188]{2,1,0:T(4,128)} %copy.45), channel_id=1, source_target_pairs={{0,8},{8,16},{16,24},{1,9},{9,17},{17,25},{2,10},{10,18},{18,26},{... | collective-permute-start | bytes 108296 | tf_op jit(solution)/shard_map/ppermute | solution.py:18
  440.8 9.4 %collective-permute-start.3 = (f32[12,4,188]{2,1,0:T(4,128)}, f32[12,4,188]{2,1,0:T(4,128)}, u32[]{:S(2)}, u32[]{:S(2)}) collective-permute-start(f32[12,4,188]{2,1,0:T(4,128)} %copy.46), channel_id=1, source_target_pairs={{8,0},{16,8},{24,16},{9,1},{17,9},{25,17},{10,2},{18,10},{26,18},{... | collective-permute-start | bytes 108296 | tf_op jit(solution)/shard_map/ppermute | solution.py:19
  452.5 1.4 copy-start
  459.7 2.1 copy-start.3
  459.7 2.1 copy-start.4
  459.7 2.1 copy-start.5
  459.7 2.1 copy-start.6
Sparse Core Ops, SparseCore 0:
  10.1 38.2 all-gather.1
  314.1 107.8 all-reduce.1
where the time goes:
time: 474 us; the launch traced here: 473 us
  waiting for transfers between devices  292 us (62%)
  local copies, waits for them, and re-layouts  84.6 us (18%)
  other arithmetic  31.8 us (7%)
  matrix products  23 us (5%)
  starting transfers between devices  16 us (3%)
  between operations  14.3 us (3%)
  blocking collectives  10.5 us (2%)
    all_to_all x1, waiting for transfers between devices, per_device(): lax.all_to_all(along_lon, 'lat', split_axis=3, concat_axis=0, tiled=True)  150 us
    psum x1, waiting for transfers between devices, per_device(): lax.psum(jnp.sum(localized * pert_rows.astype(jnp.float32), axis=1) * ens...  102 us
    all_gather x1, waiting for transfers between devices, per_device(): lax.all_gather(lon_loc, 'mem', axis=1, tiled=True)  38.8 us
    convert_element_type x1, local copies, waits for them, and re-layouts, per_device(): along_lon = jnp.einsum('mfal,lc->amfc', control, lax.all_gather(lon_loc,...  16.8 us
    dot_general x1, matrix products, per_device(): jnp.einsum('mfal,lc->amfc', control, lax.all_gather(lon_loc, 'mem', axis=...  13.5 us
    unnamed x22, local copies, waits for them, and re-layouts  12.6 us
    reshape x1, local copies, waits for them, and re-layouts, per_device(): flat_band = banded.reshape(banded.shape[0], mem_here * fields * lon_width)  12.2 us
    dot_general x1, local copies, waits for them, and re-layouts, per_device(): jnp.dot(lat_weights_all, flat_band, preferred_element_type=jnp.float32)  11.8 us
  transfers between devices with their start and end apart: 7, of which 4 were waited for; matrix products, arithmetic and copies ran while one was open for 3% of the time, Pallas kernels for 0%

commit v1 on v0

--- a/solution.py
+++ b/solution.py
@@ -3,6 +3,7 @@
 import jax.numpy as jnp
 from jax import lax
 from jax.sharding import PartitionSpec as P
+from jax.lax import axis_index, ppermute, psum
 
 NLAT = 704
 STEPS = 4
@@ -60,11 +61,31 @@
 
 
 def per_device(control, perturb, lon_loc, lat_loc, static_scale, static_field, courant):
-    along_lon = jnp.einsum(
-        "mfal,lc->amfc",
-        control,
-        lax.all_gather(lon_loc, "mem", axis=1, tiled=True),
-        preferred_element_type=jnp.float32,
+
+    def resolve_words_for(incoming_x, in_array):
+        mesh_ax = "mem"
+        carry_in = psum(1, mesh_ax)
+        t1 = axis_index(mesh_ax)
+        step_out, w_next, z2 = (carry_in, t1, incoming_x.shape[1])
+        ledger = []
+        for pp in range(step_out):
+            kept_arr = (
+                ppermute(incoming_x, mesh_ax, [(k, (k + 1) % step_out) for k in range(step_out)])
+                if pp + 1 < step_out
+                else incoming_x
+            )
+            new = in_array(incoming_x, (w_next - pp) % step_out * z2)
+            ledger.append(new)
+            incoming_x = kept_arr
+        a_now = jnp.concatenate(ledger[::-1], 3)
+        tall = jnp.roll(a_now, shift=(w_next + 1) * ledger[0].shape[3], axis=3)
+        return tall
+
+    along_lon = resolve_words_for(
+        lon_loc,
+        lambda shard_2, at: jnp.einsum(
+            "mfal,lc->amfc", control, shard_2, preferred_element_type=jnp.float32
+        ),
     ).astype(jnp.bfloat16)
     banded = lax.all_to_all(along_lon, "lat", split_axis=3, concat_axis=0, tiled=True)
     mem_here = banded.shape[1]

time: 474 us -> 495 us (1.044)
  local copies, waits for them, and re-layouts: 84.6 us -> 107 us
  waiting for transfers between devices: 292 us -> 275 us
  starting transfers between devices: 16 us -> 23.8 us
  matrix products: 23 us -> 29 us
    all_gather x1 -> x0, waiting for transfers between devices: 38.8 us -> none  [per_device(): lax.all_gather(lon_loc, 'mem', axis=1, tiled=True)]
    ppermute x0 -> x3, waiting for transfers between devices: none -> 22.2 us  [resolve_words_for(): ppermute(incoming_x, mesh_ax, [(k, (k + 1) % step_out) for k in range(ste...]
    concatenate x0 -> x1, local copies, waits for them, and re-layouts: none -> 16.7 us  [resolve_words_for(): tall = jnp.roll(a_now, shift=(w_next + 1) * ledger[0].shape[3], axis=3)]
    convert_element_type x1 -> x2, local copies, waits for them, and re-layouts: 16.8 us -> 24.8 us  [per_device(): along_lon = resolve_words_for(lon_loc, lambda shard_2, at: jnp.einsum('mf...]
    ppermute x0 -> x3, starting transfers between devices: none -> 7.6 us  [resolve_words_for(): ppermute(incoming_x, mesh_ax, [(k, (k + 1) % step_out) for k in range(ste...]
    dot_general x1 -> x4, matrix products: 13.5 us -> 19.4 us  [per_device(): jnp.einsum('mfal,lc->amfc', control, shard_2, preferred_element_type=jnp....]
    unnamed x22 -> x25, local copies, waits for them, and re-layouts: 12.6 us -> 10.2 us
  transfers between devices with their start and end apart: 7 -> 9, of which waited for: 4 -> 6; matrix products, arithmetic and copies ran while one was open for 3% -> 6% of each run, Pallas kernels for 0% -> 0%
where the time goes in v1:
time: 495 us; the launch traced here: 492 us
  waiting for transfers between devices  275 us (56%)
  local copies, waits for them, and re-layouts  107 us (22%)
  other arithmetic  31.9 us (6%)
  matrix products  29 us (6%)
  starting transfers between devices  23.8 us (5%)
  between operations  14.3 us (3%)
  blocking collectives  11.8 us (2%)
    all_to_all x1, waiting for transfers between devices, per_device(): lax.all_to_all(along_lon, 'lat', split_axis=3, concat_axis=0, tiled=True)  148 us
    psum x1, waiting for transfers between devices, per_device(): lax.psum(jnp.sum(localized * pert_rows.astype(jnp.float32), axis=1) * ens...  103 us
    convert_element_type x2, local copies, waits for them, and re-layouts, per_device(): along_lon = resolve_words_for(lon_loc, lambda shard_2, at: jnp.einsum('mf...  24.8 us
    ppermute x3, waiting for transfers between devices, resolve_words_for(): ppermute(incoming_x, mesh_ax, [(k, (k + 1) % step_out) for k in range(ste...  22.2 us
    dot_general x4, matrix products, per_device(): jnp.einsum('mfal,lc->amfc', control, shard_2, preferred_element_type=jnp....  19.4 us
    concatenate x1, local copies, waits for them, and re-layouts, resolve_words_for(): tall = jnp.roll(a_now, shift=(w_next + 1) * ledger[0].shape[3], axis=3)  16.7 us
    reshape x1, local copies, waits for them, and re-layouts, per_device(): flat_band = banded.reshape(banded.shape[0], mem_here * fields * lon_width)  12.2 us
    dot_general x1, local copies, waits for them, and re-layouts, per_device(): jnp.dot(lat_weights_all, flat_band, preferred_element_type=jnp.float32)  11.8 us
  transfers between devices with their start and end apart: 9, of which 6 were waited for; matrix products, arithmetic and copies ran while one was open for 6% of the time, Pallas kernels for 0%

profile of v1, /device:TPU:1, one launch (start us, length us, event | category | flops | bytes accessed | tf_op | source)
XLA Modules:
  0.0 492.3 jit_solution(2997312853463837)
XLA Ops:
  7.2 2.6 collective-permute-start
  9.8 12.7 %collective-permute-done = bf16[1440,360]{1,0:T(8,128)(2,1)S(1)} collective-permute-done((bf16[1440,360]{1,0:T(8,128)(2,1)}, bf16[1440,360]{1,0:T(8,128)(2,1)S(1)}, u32[]{:S(2)}, u32[]{:S(2)}) %collective-permute-start) | collective-permute-done | bytes 1036832 | tf_op jit(solution)/shard_map/ppermute | solution.py:73
  22.5 2.4 collective-permute-start.1
  24.9 6.0 %convolution_bitcast_fusion.1 = bf16[88,2,10,360]{3,0,2,1:T(8,128)(2,1)S(1)} fusion(bf16[2,10,88,1440]{3,2,1,0:T(8,128)(2,1)} %param.7, bf16[1440,360]{1,0:T(8,128)(2,1)} %param.9), kind=kOutput, calls=%fused_computation.57 | convolution fusion | flops 1824768000 | bytes 7372800 | tf_op jit(solution)/shard_map/mfal,lc->amfc/dot_general | solution.py:86
  30.8 6.4 %collective-permute-done.1 = bf16[1440,360]{1,0:T(8,128)(2,1)} collective-permute-done((bf16[1440,360]{1,0:T(8,128)(2,1)S(1)}, bf16[1440,360]{1,0:T(8,128)(2,1)}, u32[]{:S(2)}, u32[]{:S(2)}) %collective-permute-start.1) | collective-permute-done | bytes 1036832 | tf_op jit(solution)/shard_map/ppermute | solution.py:73
  37.2 2.6 collective-permute-start.2
  39.8 4.3 convolution_bitcast_fusion.2
  44.1 5.2 %convolution_bitcast_fusion.3 = bf16[88,2,10,360]{3,0,2,1:T(8,128)(2,1)} fusion(bf16[2,10,88,1440]{3,2,1,0:T(8,128)(2,1)S(1)} %copy-done.8, bf16[1440,360]{1,0:T(8,128)(2,1)} %collective-permute-done.1), kind=kOutput, calls=%fused_computation.59 | convolution fusion | flops 1824768000 | bytes 7372800 | tf_op jit(solution)/shard_map/mfal,lc->amfc/dot_general | solution.py:86
  49.3 3.1 collective-permute-done.2
  52.5 4.0 convolution_bitcast_fusion.4
  56.4 16.7 %concatenate.15 = bf16[88,2,10,2880]{3,0,2,1:T(8,128)(2,1)} concatenate(bf16[88,2,10,360]{3,0,2,1:T(8,128)(2,1)} %convolution_bitcast_fusion.4, bf16[88,2,10,360]{3,0,2,1:T(8,128)(2,1)} %convolution_bitcast_fusion.3, bf16[88,2,10,360]{3,0,2,1:T(8,128)(2,1)S(1)} %convolution_bitcast_fusion.2, bf16[88,2,10,360]{3,0,2,1:T(8,128)(2,1)S(1)} %convolution_bitcast_fusion.1, ...), dimensions={3} | concatenate | bytes 20275200 | tf_op jit(solution)/shard_map/jit(_roll_dynamic)/concatenate | solution.py:81
  73.2 7.9 %dynamic-slice_convert_fusion = bf16[88,2,10,1440]{3,0,2,1:T(8,128)(2,1)} fusion(bf16[88,2,10,2880]{3,0,2,1:T(8,128)(2,1)} %concatenate.15, s32[]{:T(128)S(6)} %select_n.17), kind=kLoop, calls=%fused_computation.2 | loop fusion | bytes 10137604 | tf_op jit(solution)/shard_map/convert_element_type | solution.py:89
  81.1 16.8 %copy.30 = bf16[88,2,10,1440]{0,1,2,3:T(2,128)(2,1)} copy(bf16[88,2,10,1440]{3,0,2,1:T(8,128)(2,1)} %dynamic-slice_convert_fusion) | data formatting | bytes 10137600 | tf_op jit(solution)/shard_map/convert_element_type | solution.py:89
  98.0 5.7 %all-to-all-start = ((bf16[88,2,10,1440]{0,1,2,3:T(2,128)(2,1)}), bf16[88,2,10,1440]{0,1,2,3:T(2,128)(2,1)}, u32[]{:S(2)}, u32[]{:S(2)}) async-start(bf16[88,2,10,1440]{0,1,2,3:T(2,128)(2,1)} %copy.30), calls=%async_computation | async-start | bytes 14745600 | tf_op jit(solution)/shard_map/all_to_all | solution.py:90
  103.7 11.8 %all_gather.3 = bf16[704,704]{1,0:T(8,128)(2,1)S(1)} all-gather(bf16[176,704]{1,0:T(8,128)(2,1)S(1)} %copy-done.7), channel_id=1, replica_groups=mesh['mem'=4,'lat'=8] {'mem'}, dimensions={0}, use_global_device_ids=true | all-gather | bytes 1239040 | tf_op jit(solution)/shard_map/all_gather | solution.py:96
  115.5 148.1 %all-to-all-done = bf16[88,2,10,1440]{0,1,2,3:T(2,128)(2,1)} async-done(((bf16[88,2,10,1440]{0,1,2,3:T(2,128)(2,1)}), bf16[88,2,10,1440]{0,1,2,3:T(2,128)(2,1)}, u32[]{:S(2)}, u32[]{:S(2)}) %all-to-all-start) | async-done | bytes 5068832 | tf_op jit(solution)/shard_map/all_to_all | solution.py:90
  263.6 8.0 %copy.57 = bf16[88,2,10,8,180]{0,3,4,2,1:T(8,128)(2,1)} copy(bf16[88,2,10,8,180]{0,1,2,4,3:T(2,128)(2,1)} %bitcast.12) | data formatting | bytes 10137600 | tf_op jit(solution)/shard_map/all_to_all | solution.py:90
  271.6 12.2 %reshape.11 = bf16[704,3600]{0,1:T(8,128)(2,1)} reshape(bf16[8,88,2,10,180]{1,0,4,3,2:T(8,128)(2,1)} %bitcast.84) | data formatting | bytes 10137600 | tf_op jit(solution)/shard_map/reshape | solution.py:94
  283.8 9.6 %convolution_bitcast_fusion = f32[704,3600]{1,0:T(8,128)} fusion(bf16[704,3600]{0,1:T(8,128)(2,1)} %reshape.11, bf16[704,704]{1,0:T(8,128)(2,1)S(1)} %all_gather.3), kind=kOutput, calls=%fused_computation.4 | convolution fusion | flops 3568435200 | bytes 16197632 | tf_op jit(solution)/shard_map/dot_general | solution.py:100
  293.4 11.8 %copy.32 = f32[704,3600]{0,1:T(8,128)} copy(f32[704,3600]{1,0:T(8,128)} %convolution_bitcast_fusion) | data formatting | bytes 20275200 | tf_op jit(solution)/shard_map/dot_general | solution.py:100
  305.2 11.6 %reshape.12 = f32[704,2,10,180]{0,3,2,1:T(8,128)} reshape(f32[704,3600]{0,1:T(8,128)} %copy.32) | data formatting | bytes 20275200 | tf_op jit(solution)/shard_map/reshape | solution.py:101
  316.8 10.3 %fusion = f32[704,10,180]{0,2,1:T(8,128)} fusion(f32[704,2,10,180]{0,3,2,1:T(8,128)} %reshape.12, bf16[2,10,704,180]{2,0,3,1:T(2,128)(2,1)} %param.8), kind=kLoop, calls=%fused_computation.1 | loop fusion | flops 6336000 | bytes 20275200 | tf_op jit(solution)/shard_map/reduce_sum | solution.py:103
  327.1 5.5 %broadcast_multiply_fusion = f32[704,10,180]{0,2,1:T(8,128)} fusion(f32[704,10,180]{0,2,1:T(8,128)} %fusion), kind=kLoop, calls=%fused_computation.5 | loop fusion | flops 1267200 | bytes 10137600 | tf_op jit(solution)/shard_map/mul | solution.py:103
  335.9 3.0 copy.35
  339.1 102.6 %all-reduce.2.cloned.1.call-done = f32[704,10,180]{0,2,1:T(8,128)} async-done(((f32[704,10,180]{0,2,1:T(8,128)}), f32[704,10,180]{0,2,1:T(8,128)}) %all-reduce.2.cloned.1.call-update) | async-done | bytes 5068816 | tf_op jit(solution)/shard_map/psum | solution.py:103
  441.7 3.5 bitcast_add_fusion
  446.5 3.0 collective-permute-start.4
  452.9 2.4 copy.41
  455.3 4.1 collective-permute-start.5
  460.5 2.1 collective-permute-start.6
  469.9 2.2 copy.44
  475.3 2.1 fusion.3
  (55 shorter events, 27.6 us)
Async XLA Ops:
  7.2 15.3 %collective-permute-start = (bf16[1440,360]{1,0:T(8,128)(2,1)}, bf16[1440,360]{1,0:T(8,128)(2,1)S(1)}, u32[]{:S(2)}, u32[]{:S(2)}) collective-permute-start(bf16[1440,360]{1,0:T(8,128)(2,1)} %param.9), channel_id=1, source_target_pairs={{0,8},{8,16},{16,24},{24,0},{1,9},{9,17},{17,25},{25,1},{2,10},{10... | collective-permute-start | bytes 3110408 | tf_op jit(solution)/shard_map/ppermute | solution.py:73
  22.5 8.4 %copy-start.9 = (bf16[1440,360]{1,0:T(8,128)(2,1)}, bf16[1440,360]{1,0:T(8,128)(2,1)S(1)}, u32[]{:S(2)}) copy-start(bf16[1440,360]{1,0:T(8,128)(2,1)S(1)} %collective-permute-done) | copy-start | bytes 3110404
  22.5 14.7 %collective-permute-start.1 = (bf16[1440,360]{1,0:T(8,128)(2,1)S(1)}, bf16[1440,360]{1,0:T(8,128)(2,1)}, u32[]{:S(2)}, u32[]{:S(2)}) collective-permute-start(bf16[1440,360]{1,0:T(8,128)(2,1)S(1)} %collective-permute-done), channel_id=1, source_target_pairs={{0,8},{8,16},{16,24},{24,0},{1,9},{9,17},{17,25},{25,1},{2,10},{10... | collective-permute-start | bytes 3110408 | tf_op jit(solution)/shard_map/ppermute | solution.py:73
  24.9 14.9 %copy-start.8 = (bf16[2,10,88,1440]{3,2,1,0:T(8,128)(2,1)S(1)}, bf16[2,10,88,1440]{3,2,1,0:T(8,128)(2,1)}, u32[]{:S(2)}) copy-start(bf16[2,10,88,1440]{3,2,1,0:T(8,128)(2,1)} %param.7) | copy-start | bytes 15206404
  37.2 15.3 %collective-permute-start.2 = (bf16[1440,360]{1,0:T(8,128)(2,1)}, bf16[1440,360]{1,0:T(8,128)(2,1)S(1)}, u32[]{:S(2)}, u32[]{:S(2)}) collective-permute-start(bf16[1440,360]{1,0:T(8,128)(2,1)} %collective-permute-done.1), channel_id=1, source_target_pairs={{0,8},{8,16},{16,24},{24,0},{1,9},{9,17},{17,25},{25,1},{2,10},{10... | collective-permute-start | bytes 3110408 | tf_op jit(solution)/shard_map/ppermute | solution.py:73
  98.0 5.7 %copy-start.7 = (bf16[176,704]{1,0:T(8,128)(2,1)S(1)}, bf16[176,704]{1,0:T(8,128)(2,1)}, u32[]{:S(2)}) copy-start(bf16[176,704]{1,0:T(8,128)(2,1)} %param.10) | copy-start | bytes 743428
  98.0 165.7 %all-to-all-start = ((bf16[88,2,10,1440]{0,1,2,3:T(2,128)(2,1)}), bf16[88,2,10,1440]{0,1,2,3:T(2,128)(2,1)}, u32[]{:S(2)}, u32[]{:S(2)}) async-start(bf16[88,2,10,1440]{0,1,2,3:T(2,128)(2,1)} %copy.30), calls=%async_computation | async-start | bytes 14745600 | tf_op jit(solution)/shard_map/all_to_all | solution.py:90
  103.6 338.1 %all-reduce.2.cloned.1.call-start = ((), (), s32[]{:S(2)}) async-start(), calls=%async_computation.1 | async-start | bytes 11304960 | tf_op jit(solution)/shard_map/psum | solution.py:103
  332.6 1.5 copy-start.1
  335.9 3.0 copy-start.2
  445.2 5.9 %collective-permute-start.3 = (f32[12,176,4]{1,0,2:T(8,128)S(1)}, f32[12,176,4]{1,0,2:T(8,128)S(1)}, u32[]{:S(2)}, u32[]{:S(2)}) collective-permute-start(f32[12,176,4]{1,0,2:T(8,128)S(1)} %copy.37), channel_id=1, source_target_pairs={{0,1},{1,2},{2,3},{3,4},{4,5},{5,6},{6,7},{7,0},{8,9},{9,10},{10,1... | collective-permute-start | bytes 101384 | tf_op jit(solution)/shard_map/ppermute | solution.py:19
  446.5 4.7 collective-permute-start.4
  455.3 13.4 %collective-permute-start.5 = (f32[12,4,188]{2,1,0:T(4,128)}, f32[12,4,188]{2,1,0:T(4,128)}, u32[]{:S(2)}, u32[]{:S(2)}) collective-permute-start(f32[12,4,188]{2,1,0:T(4,128)} %copy.41), channel_id=1, source_target_pairs={{0,8},{8,16},{16,24},{1,9},{9,17},{17,25},{2,10},{10,18},{18,26},{... | collective-permute-start | bytes 108296 | tf_op jit(solution)/shard_map/ppermute | solution.py:19
  460.5 9.4 %collective-permute-start.6 = (f32[12,4,188]{2,1,0:T(4,128)}, f32[12,4,188]{2,1,0:T(4,128)}, u32[]{:S(2)}, u32[]{:S(2)}) collective-permute-start(f32[12,4,188]{2,1,0:T(4,128)} %copy.42), channel_id=1, source_target_pairs={{8,0},{16,8},{24,16},{9,1},{17,9},{25,17},{10,2},{18,10},{26,18},{... | collective-permute-start | bytes 108296 | tf_op jit(solution)/shard_map/ppermute | solution.py:20
  472.2 1.4 copy-start
  479.4 2.1 copy-start.3
  479.4 2.1 copy-start.4
  479.4 2.1 copy-start.5
  479.4 2.1 copy-start.6
Sparse Core Ops, SparseCore 0:
  332.8 108.8 all-reduce.1
